TPU v7x, 32 devices: a whole 2x2x4 slice. The times are simulated.
32 devices in a mesh: cp: 8 (over z, x), tp: 4 (over y, core).
Axes of the slice: x: 2, y: 2, z: 4, core: 2. Of those that a mesh axis runs over, the one named last changes fastest.
Arguments:
- queries: bfloat16 [1024, 8192], P('cp', 'tp'), may hold values from -6 to 6
- keys: bfloat16 [1024, 1024], P('cp', 'tp'), may hold values from -6 to 6
- values: bfloat16 [1024, 1024], P('cp', 'tp'), may hold values from -6 to 6
- doc_blocks: int32 [4], replicated, may hold values from 1 to 4, 8 in all
- block_order: int32 [8], replicated, may hold values from 0 to 7, each once
- out_weight: bfloat16 [8192, 4096], P('tp'), may hold values from -0.5 to 0.5
Outputs:
- layer_out: bfloat16 [1024, 4096], P(('cp', 'tp'))
Inputs may be any that keep to these rules, and one draw needn't show every extreme that they name: Array block i (rows i * 128 to i * 128 + 127) holds sequence block block_order[i]; every block number appears once. `doc_blocks`: they sum to 8; the longest document has exactly 4 blocks.
All inputs are finite; a program needn't handle non-finite values.
Results may differ from a plain program's by a relative error of at most 0.013.
Values may be sent and summed in bfloat16 or wider, within the bound.
A program may use at most 128 MiB of HBM per device.

v0:
```python
import functools

import jax
import jax.numpy as jnp
from jax import lax
from jax.experimental import pallas as pl
from jax.experimental.pallas import tpu as pltpu
from jax.sharding import PartitionSpec as P

HEAD_SIZE = 128
BLOCK_TOKENS = 128
MASKED = -1e30
LOG2E = 1.4426950408889634
MESH = pl.DeviceIdType.MESH


def kernel(
    nc, ndoc, chunks,
    q_hbm, k_hbm, v_hbm, doc_ref, ord_ref, w_hbm, o_hbm,
    w_v, q_v, kv, m_s, acc, att, p_v, r1, s2, r2, o_v,
    kv_sem, q_sem, w_sem, dn_send, z_send, x_send, ag_recv, c_send, c_recv, y_send, y_recv, o_sem,
):
    D = HEAD_SIZE
    me = lax.axis_index("cp")
    tp = lax.axis_index("tp")
    core = lax.rem(tp, 2)
    yy = lax.div(tp, 2)
    sib = yy * 2 + (1 - core)
    ypeer = (1 - yy) * 2 + core
    cz = nc // 2
    z = lax.div(me, 2)
    x = lax.rem(me, 2)
    heads_kv = kv.shape[1]
    group = q_v.shape[1] // (heads_kv * D)
    width = w_v.shape[2]

    local = []
    for h in range(heads_kv):
        for i, src in enumerate((k_hbm, v_hbm)):
            local.append(pltpu.make_async_copy(
                src.at[:, pl.ds(h * D, D)], kv.at[me, h, i], kv_sem.at[2 * h + i]))
    for c in local:
        c.start()
    q_copy = pltpu.make_async_copy(q_hbm, q_v, q_sem)
    q_copy.start()

    def w_copy(c):
        return pltpu.make_async_copy(
            w_hbm.at[:, pl.ds(c * width, width)], w_v.at[c], w_sem.at[c])

    barrier = pltpu.get_barrier_semaphore()

    has_up, has_dn = z + 1 < cz, z > 0
    nb = z * 2 + (1 - x)

    def greet(where):
        pl.semaphore_signal(barrier, inc=1, device_id=where, device_id_type=MESH)

    pl.when(has_up)(lambda: greet({"cp": me + 2}))
    pl.when(has_dn)(lambda: greet({"cp": me - 2}))
    greet({"cp": nb})
    greet({"tp": sib})
    greet({"tp": ypeer})
    pl.semaphore_wait(barrier, 3 + jnp.where(has_up, 1, 0) + jnp.where(has_dn, 1, 0))

    def hop(b, h, dst, sem):
        return pltpu.make_async_remote_copy(
            src_ref=kv.at[b, h], dst_ref=kv.at[b, h],
            send_sem=sem, recv_sem=ag_recv.at[b, h],
            device_id={"cp": dst}, device_id_type=MESH)

    def own_up(h):
        return hop(me, h, me + 2, z_send.at[me, h])

    def own_dn(h):
        return hop(me, h, me - 2, dn_send.at[h])

    def over_x(b, h):
        return hop(b, h, nb, x_send.at[b, h])

    def over_z(b, h, dst):
        return hop(b, h, dst, z_send.at[b, h])

    for h in range(heads_kv):
        local[2 * h].wait()
        local[2 * h + 1].wait()
        pl.when(has_up)(lambda: own_up(h).start())
        pl.when(has_dn)(lambda: own_dn(h).start())
        over_x(me, h).start()

    early = 2
    for c in range(early):
        w_copy(c).start()

    left, right = z, cz - 1 - z
    near = jnp.where(left < right, left, right)
    far_side = jnp.where(left < right, 1, -1)

    def nearest(j):
        both = j <= 2 * near
        side = jnp.where(both, 2 * lax.rem(j, 2) - 1, far_side)
        zz = z + side * jnp.where(both, lax.div(j + 1, 2), j - near)
        return zz * 2 + x, zz * 2 + (1 - x), z - side

    ends = []
    total = 0
    for d in range(ndoc):
        total = total + doc_ref[d]
        ends.append(total)

    def place(b):
        s = ord_ref[b]
        doc = jnp.int32(0)
        for e in ends:
            doc = doc + jnp.where(s >= e, 1, 0).astype(jnp.int32)
        return s, doc

    s0, d0 = place(me)

    def bias_of(b):
        s, doc = place(b)
        return jnp.where((doc == d0) & (s < s0), 0.0, MASKED).astype(jnp.float32)

    scale = HEAD_SIZE ** -0.5 * LOG2E
    tile = 2 * BLOCK_TOKENS
    col = lax.broadcasted_iota(jnp.int32, (tile, tile), 1)
    row = lax.broadcasted_iota(jnp.int32, (tile, tile), 0)
    col1 = lax.broadcasted_iota(jnp.int32, (1, tile), 1)
    ones = jnp.ones((tile, D), jnp.bfloat16)

    def step(b0, b1, bias, first, heads):
        for h in heads:
            k2 = jnp.concatenate([kv[b0, h, 0], kv[b1, h, 0]], axis=0)
            v2 = jnp.concatenate([kv[b0, h, 1], kv[b1, h, 1]], axis=0)
            v2 = jnp.concatenate([v2, ones], axis=1)
            for t in range(group // 2):
                hq = h * group + 2 * t
                q2 = jnp.concatenate(
                    [q_v[:, hq * D:(hq + 1) * D], q_v[:, (hq + 1) * D:(hq + 2) * D]], axis=0)
                s = lax.dot_general(
                    q2, k2, (((1,), (1,)), ((), ())), preferred_element_type=jnp.float32)
                s = s * scale + bias
                top = jnp.max(s, axis=1, keepdims=True)
                rows = pl.ds(hq * BLOCK_TOKENS, tile)
                if first:
                    m_new = top
                else:
                    m_old = m_s[rows, 0:1]
                    m_new = jnp.maximum(m_old, top)
                p = jnp.exp2(s - m_new).astype(jnp.bfloat16)
                pv = jnp.dot(p, v2, preferred_element_type=jnp.float32)
                if first:
                    acc[rows, :] = pv
                else:
                    acc[rows, :] = acc[rows, :] * jnp.exp2(m_old - m_new) + pv
                m_s[rows, :] = jnp.broadcast_to(m_new, (tile, D))

    inside = row - jnp.where(row >= BLOCK_TOKENS, BLOCK_TOKENS, 0)
    bias0 = jnp.where(
        col >= BLOCK_TOKENS, bias_of(nb), jnp.where(col <= inside, 0.0, MASKED))

    def pass_on(j, h):
        b, _, nxt = nearest(j)
        over_x(b, h).wait_recv()
        pl.when((nxt >= 0) & (nxt < cz))(lambda: over_z(b, h, nxt * 2 + x).start())
        over_x(b, h).start()
        c = early + (j - 1) * heads_kv + h
        pl.when(c < chunks)(lambda: w_copy(c).start())

    def attend(j, h):
        b0, b1, _ = nearest(j)
        bias = jnp.where(col1 >= BLOCK_TOKENS, bias_of(b1), bias_of(b0))
        over_x(b1, h).wait_recv()
        step(b0, b1, bias, False, (h,))

    q_copy.wait()
    for h in range(heads_kv):
        pass_on(1, h)
        over_x(nb, h).wait_recv()
        step(me, nb, bias0, True, (h,))

    @pl.loop(2, cz)
    def _(j):
        for h in range(heads_kv):
            pass_on(j, h)
            attend(j - 1, h)

    for c in range(min(chunks, early + (cz - 1) * heads_kv), chunks):
        w_copy(c).start()
    for h in range(heads_kv):
        attend(cz - 1, h)

    for hq in range(heads_kv * group):
        rows = pl.ds(hq * BLOCK_TOKENS, BLOCK_TOKENS)
        att[:, hq * D:(hq + 1) * D] = (acc[rows, :D] / acc[rows, D:]).astype(jnp.bfloat16)

    strip = BLOCK_TOKENS // 4

    def c_copy(c):
        return pltpu.make_async_remote_copy(
            src_ref=p_v.at[c, 1 - core], dst_ref=r1.at[c],
            send_sem=c_send.at[c], recv_sem=c_recv.at[c],
            device_id={"tp": sib}, device_id_type=MESH)

    def y_copy(c):
        return pltpu.make_async_remote_copy(
            src_ref=s2.at[c], dst_ref=r2.at[c],
            send_sem=y_send.at[c], recv_sem=y_recv.at[c],
            device_id={"tp": ypeer}, device_id_type=MESH)

    def o_copy(c):
        return pltpu.make_async_copy(
            o_v.at[c], o_hbm.at[:, pl.ds(c * width, width)], o_sem.at[c])

    def stage1(c):
        w_copy(c).wait()
        part = jnp.dot(att[...], w_v[c], preferred_element_type=jnp.float32)
        part = part.astype(jnp.bfloat16)
        for t in range(4):
            p_v[c, t % 2, t // 2] = part[t * strip:(t + 1) * strip]
        c_copy(c).start()

    def stage2(c):
        c_copy(c).wait_recv()
        s2[c] = (p_v[c, core, 1 - yy].astype(jnp.float32)
                 + r1[c, 1 - yy].astype(jnp.float32)).astype(jnp.bfloat16)
        y_copy(c).start()

    def stage3(c):
        y_copy(c).wait_recv()
        o_v[c] = (p_v[c, core, yy].astype(jnp.float32) + r1[c, yy].astype(jnp.float32)
                  + r2[c].astype(jnp.float32)).astype(jnp.bfloat16)
        o_copy(c).start()

    lag2, lag3 = 1, 5
    for i in range(chunks + lag3):
        if i < chunks:
            stage1(i)
        if 0 <= i - lag2 < chunks:
            stage2(i - lag2)
        if 0 <= i - lag3 < chunks:
            stage3(i - lag3)

    for h in range(heads_kv):
        pl.when(has_up)(lambda: own_up(h).wait_send())
        pl.when(has_dn)(lambda: own_dn(h).wait_send())
        over_x(me, h).wait_send()

    @pl.loop(1, cz)
    def _(j):
        b, _, nxt = nearest(j)
        for h in range(heads_kv):
            pl.when((nxt >= 0) & (nxt < cz))(lambda: over_z(b, h, nxt * 2 + x).wait_send())
            over_x(b, h).wait_send()

    for c in range(chunks):
        c_copy(c).wait_send()
        y_copy(c).wait_send()
        o_copy(c).wait()


def local_fn(nc, queries, keys, values, doc_blocks, block_order, out_weight):
    rows, qcols = queries.shape
    depth, cols = out_weight.shape
    heads_kv = keys.shape[1] // HEAD_SIZE
    chunks = 8
    width = cols // chunks
    strip = rows // 4
    bf, f32 = jnp.bfloat16, jnp.float32
    dma = pltpu.SemaphoreType.DMA
    anyspec = pl.BlockSpec(memory_space=pl.ANY)
    smem = pl.BlockSpec(memory_space=pltpu.SMEM)
    return pl.pallas_call(
        functools.partial(kernel, nc, doc_blocks.shape[0], chunks),
        out_shape=jax.ShapeDtypeStruct((strip, cols), bf),
        in_specs=[anyspec, anyspec, anyspec, smem, smem, anyspec],
        out_specs=anyspec,
        scratch_shapes=[
            pltpu.VMEM((chunks, depth, width), bf),
            pltpu.VMEM((rows, qcols), bf),
            pltpu.VMEM((nc, heads_kv, 2, BLOCK_TOKENS, HEAD_SIZE), bf),
            pltpu.VMEM((qcols, HEAD_SIZE), f32),
            pltpu.VMEM((qcols, 2 * HEAD_SIZE), f32),
            pltpu.VMEM((rows, qcols), bf),
            pltpu.VMEM((chunks, 2, 2, strip, width), bf),
            pltpu.VMEM((chunks, 2, strip, width), bf),
            pltpu.VMEM((chunks, strip, width), bf),
            pltpu.VMEM((chunks, strip, width), bf),
            pltpu.VMEM((chunks, strip, width), bf),
            dma((2 * heads_kv,)), dma, dma((chunks,)),
            dma((heads_kv,)), dma((nc, heads_kv)), dma((nc, heads_kv)), dma((nc, heads_kv)),
            dma((chunks,)), dma((chunks,)), dma((chunks,)), dma((chunks,)), dma((chunks,)),
        ],
        compiler_params=pltpu.CompilerParams(
            collective_id=0, has_side_effects=True, vmem_limit_bytes=60 * 2**20),
    )(queries, keys, values, doc_blocks, block_order, out_weight)


def solution(mesh):
    placed = (P("cp", "tp"), P("cp", "tp"), P("cp", "tp"), P(), P(), P("tp", None))
    assert mesh.shape["tp"] == 4
    return jax.shard_map(
        functools.partial(local_fn, mesh.shape["cp"]),
        mesh=mesh, in_specs=placed, out_specs=P(("cp", "tp"), None), check_vma=False,
    )
```

profile of v0, /device:TPU:0, one launch (start us, length us, event | category | flops | bytes accessed | tf_op | source)
XLA Modules:
  0.0 39.6 jit_solution(5571900879660909384)
XLA Ops:
  0.0 37.9 %shard_map.64 = bf16[32,4096]{1,0:T(8,128)(2,1)} custom-call(bf16[128,2048]{1,0:T(8,128)(2,1)} %q_hbm.1, bf16[128,256]{1,0:T(8,128)(2,1)} %k_hbm.1, bf16[128,256]{1,0:T(8,128)(2,1)} %v_hbm.1, s32[4]{0:T(128)} %doc_ref.1, s32[8]{0:T(128)} %ord_ref.1, bf16[2048,4096]{1,0:T(8,128)(2,1)} %w_hbm.1), custom_call_target="tpu_custom_call" | custom-call | tf_op jit(solution)/shard_map/pallas_call | solution.py:273
  37.9 1.7 %copy.8 = bf16[32,4096]{1,0:T(8,128)(2,1)} copy(bf16[32,4096]{1,0:T(8,128)(2,1)} %shard_map.64) | data formatting | bytes 524288
where the time goes:
time: 39.8 us; the launch traced here: 39.6 us
  Pallas kernels  37.9 us (95%)
  local copies, waits for them, and re-layouts  1.67 us (4%)
    pallas_call x1, Pallas kernels, local_fn(): pl.pallas_call(functools.partial(kernel, nc, doc_blocks.shape[0], chunks)...  37.9 us
    unnamed x1, local copies, waits for them, and re-layouts  1.67 us

commit v1 on v0

--- a/solution.py
+++ b/solution.py
@@ -16,9 +16,9 @@
 
 def kernel(
     nc, ndoc, chunks,
-    q_hbm, k_hbm, v_hbm, doc_ref, ord_ref, w_hbm, o_hbm,
+    q_hbm, k_hbm, v_hbm, doc_hbm, ord_hbm, w_hbm, o_hbm,
     w_v, q_v, kv, m_s, acc, att, p_v, r1, s2, r2, o_v,
-    kv_sem, q_sem, w_sem, dn_send, z_send, x_send, ag_recv, c_send, c_recv, y_send, y_recv, o_sem,
+    kv_sem, q_sem, w_sem, dn_send, z_send, x_send, ag_recv, c_send, c_recv, y_send, y_recv, o_sem, doc_ref, ord_ref, s_sem,
 ):
     D = HEAD_SIZE
     me = lax.axis_index("cp")
@@ -48,6 +48,8 @@
         return pltpu.make_async_copy(
             w_hbm.at[:, pl.ds(c * width, width)], w_v.at[c], w_sem.at[c])
 
+    sc = [pltpu.make_async_copy(doc_hbm, doc_ref, s_sem.at[0]), pltpu.make_async_copy(ord_hbm, ord_ref, s_sem.at[1])]
+    for c in sc: c.start()
     barrier = pltpu.get_barrier_semaphore()
 
     has_up, has_dn = z + 1 < cz, z > 0
@@ -102,6 +104,7 @@
         zz = z + side * jnp.where(both, lax.div(j + 1, 2), j - near)
         return zz * 2 + x, zz * 2 + (1 - x), z - side
 
+    for c in sc: c.wait()
     ends = []
     total = 0
     for d in range(ndoc):
@@ -268,12 +271,13 @@
     strip = rows // 4
     bf, f32 = jnp.bfloat16, jnp.float32
     dma = pltpu.SemaphoreType.DMA
+    hbm = pl.BlockSpec(memory_space=pltpu.HBM)
     anyspec = pl.BlockSpec(memory_space=pl.ANY)
     smem = pl.BlockSpec(memory_space=pltpu.SMEM)
     return pl.pallas_call(
         functools.partial(kernel, nc, doc_blocks.shape[0], chunks),
         out_shape=jax.ShapeDtypeStruct((strip, cols), bf),
-        in_specs=[anyspec, anyspec, anyspec, smem, smem, anyspec],
+        in_specs=[hbm, hbm, hbm, hbm, hbm, hbm],
         out_specs=anyspec,
         scratch_shapes=[
             pltpu.VMEM((chunks, depth, width), bf),
@@ -289,11 +293,11 @@
             pltpu.VMEM((chunks, strip, width), bf),
             dma((2 * heads_kv,)), dma, dma((chunks,)),
             dma((heads_kv,)), dma((nc, heads_kv)), dma((nc, heads_kv)), dma((nc, heads_kv)),
-            dma((chunks,)), dma((chunks,)), dma((chunks,)), dma((chunks,)), dma((chunks,)),
+            dma((chunks,)), dma((chunks,)), dma((chunks,)), dma((chunks,)), dma((chunks,)), pltpu.SMEM(doc_blocks.shape, jnp.int32), pltpu.SMEM(block_order.shape, jnp.int32), dma((2,)),
         ],
         compiler_params=pltpu.CompilerParams(
-            collective_id=0, has_side_effects=True, vmem_limit_bytes=60 * 2**20),
-    )(queries, keys, values, doc_blocks, block_order, out_weight)
+            collective_id=0, has_side_effects=True, vmem_limit_bytes=40 * 2**20),
+    )(*[pltpu.with_memory_space_constraint(a, pltpu.HBM) for a in (queries, keys, values, doc_blocks, block_order, out_weight)])
 
 
 def solution(mesh):

time: 39.8 us -> 37.6 us (0.945)
  Pallas kernels: 37.9 us -> 36.8 us
  local copies, waits for them, and re-layouts: 1.67 us -> 0.71 us
    pallas_call x1, Pallas kernels: 37.9 us -> 36.8 us  [local_fn(): pl.pallas_call(functools.partial(kernel, nc, doc_blocks.shape[0], chunks)...]
    unnamed x1, local copies, waits for them, and re-layouts: 1.67 us -> 0.71 us
where the time goes in v1:
time: 37.6 us; the launch traced here: 37.5 us
  Pallas kernels  36.8 us (98%)
  local copies, waits for them, and re-layouts  0.71 us (2%)
    pallas_call x1, Pallas kernels, local_fn(): pl.pallas_call(functools.partial(kernel, nc, doc_blocks.shape[0], chunks)...  36.8 us

profile of v1, /device:TPU:0, one launch (start us, length us, event | category | flops | bytes accessed | tf_op | source)
XLA Modules:
  0.0 37.5 jit_solution(16702672272844024716)
XLA Ops:
  0.0 36.8 %shard_map.64 = bf16[32,4096]{1,0:T(8,128)(2,1)S(1)} custom-call(bf16[128,2048]{1,0:T(8,128)(2,1)} %q_hbm.1, bf16[128,256]{1,0:T(8,128)(2,1)} %k_hbm.1, bf16[128,256]{1,0:T(8,128)(2,1)} %v_hbm.1, s32[4]{0:T(128)} %doc_hbm.1, s32[8]{0:T(128)} %ord_hbm.1, bf16[2048,4096]{1,0:T(8,128)(2,1)} %w_hbm.1), custom_call_target="tpu_custom_call" | custom-call | tf_op jit(solution)/shard_map/pallas_call | solution.py:277
  36.8 0.7 %copy.8 = bf16[32,4096]{1,0:T(8,128)(2,1)} copy(bf16[32,4096]{1,0:T(8,128)(2,1)S(1)} %shard_map.64) | data formatting | bytes 524288

commit v2 on v0

v2 whole, which is shorter than its diff:
```python
import functools

import jax
import jax.numpy as jnp
from jax import lax
from jax.experimental import pallas as pl
from jax.experimental.pallas import tpu as pltpu
from jax.sharding import PartitionSpec as P

HEAD_SIZE = 128
BLOCK_TOKENS = 128
MASKED = -1e30
LOG2E = 1.4426950408889634
MESH = pl.DeviceIdType.MESH
GROUP_BLOCKS = 4
UNROLL = 4


def each(lo, hi, body):
    if hi - lo <= UNROLL:
        for j in range(lo, hi):
            body(j)
    else:
        pl.loop(lo, hi)(body)


def kernel(nc, ndoc, chunks, heads_kv, q_hbm, k_hbm, v_hbm, doc_hbm, ord_hbm, w_hbm, o_ref, *scratch):
    D = HEAD_SIZE
    (doc_ref, ord_ref, w_v, q_v, att, p_v, r1, s2, r2, m_s, acc,
     s_sem, kv_sem, q_sem, w_sem, up_send, dn_send, x_send, ag_recv,
     c_send, c_recv, y_send, y_recv) = scratch[:23]
    kv = scratch[23:]
    me = lax.axis_index("cp")
    tp = lax.axis_index("tp")
    core = lax.rem(tp, 2)
    yy = lax.div(tp, 2)
    sib = yy * 2 + (1 - core)
    ypeer = (1 - yy) * 2 + core
    cz = nc // 2
    z = lax.div(me, 2)
    x = lax.rem(me, 2)
    nb = z * 2 + (1 - x)
    group = q_v.shape[1] // (heads_kv * D)
    width = w_v.shape[2]
    span = nc // 2

    def buf(h, c):
        return kv[2 * h + c]

    pieces = [(h, c) for c in (1, 0) for h in range(heads_kv)]
    local = {}
    for h, c in pieces:
        local[h, c] = pltpu.make_async_copy(
            (k_hbm, v_hbm)[c].at[:, pl.ds(h * D, D)], buf(h, c).at[me], kv_sem.at[h, c])
    for h, c in pieces:
        local[h, c].start()
    small = [pltpu.make_async_copy(doc_hbm, doc_ref, s_sem.at[0]),
             pltpu.make_async_copy(ord_hbm, ord_ref, s_sem.at[1])]
    for s in small:
        s.start()
    q_copy = pltpu.make_async_copy(q_hbm, q_v, q_sem)
    q_copy.start()

    def w_copy(c):
        return pltpu.make_async_copy(
            w_hbm.at[:, pl.ds(c * width, width)], w_v.at[c], w_sem.at[c])

    barrier = pltpu.get_barrier_semaphore()
    has_up, has_dn = z + 1 < cz, z > 0

    def greet(where):
        pl.semaphore_signal(barrier, inc=1, device_id=where, device_id_type=MESH)

    pl.when(has_up)(lambda: greet({"cp": me + 2}))
    pl.when(has_dn)(lambda: greet({"cp": me - 2}))
    greet({"cp": nb})
    greet({"tp": sib})
    greet({"tp": ypeer})
    pl.semaphore_wait(barrier, 3 + jnp.where(has_up, 1, 0) + jnp.where(has_dn, 1, 0))

    def hop(b, h, c, dst, sem):
        return pltpu.make_async_remote_copy(
            src_ref=buf(h, c).at[b], dst_ref=buf(h, c).at[b],
            send_sem=sem.at[b, h, c], recv_sem=ag_recv.at[b, h, c],
            device_id={"cp": dst}, device_id_type=MESH)

    def over_x(b, h, c):
        return hop(b, h, c, nb, x_send)

    def along(b, h, c, side):
        if side > 0:
            return hop(b, h, c, me - 2, dn_send)
        return hop(b, h, c, me + 2, up_send)

    def within(level):
        return (level >= 0) & (level < cz)

    def is_end(level):
        return (level == 0) | (level == cz - 1)

    for h, c in pieces:
        local[h, c].wait()
        pl.when(has_up)(lambda: along(me, h, c, -1).start())
        pl.when(has_dn)(lambda: along(me, h, c, 1).start())
    for h, c in reversed(pieces):
        over_x(me, h, c).start()

    for c in range(chunks):
        w_copy(c).start()

    def column(d, h, c, side, act_z, act_x, wait):
        zb = z + side * d

        @pl.when(within(zb))
        def _():
            b = zb * 2 + x
            if wait:
                over_x(b, h, c).wait_recv()
            pl.when(within(z - side))(lambda: act_z(along(b, h, c, side)))
            if c == 0:
                pl.when(jnp.logical_not(is_end(zb)))(lambda: act_x(over_x(b, h, c)))
            else:
                act_x(over_x(b, h, c))

    def cross(d, h, side, act_z, wait):
        zb = z + side * d

        @pl.when(zb == (cz - 1 if side > 0 else 0))
        def _():
            b = zb * 2 + (1 - x)
            if wait:
                over_x(b, h, 0).wait_recv()
            pl.when(within(z - side))(lambda: act_z(along(b, h, 0, side)))

    def relay(d, act_z, act_x, wait):
        for i, (h, c) in enumerate(pieces):
            for side in (1, -1):
                column(d, h, c, side, act_z, act_x, wait)
            if i < heads_kv:
                for side in (1, -1):
                    cross(d - 1, i, side, act_z, wait)

    def start(copy):
        copy.start()

    def sent(copy):
        copy.wait_send()

    each(1, cz, lambda d: relay(d, start, start, True))

    for s in small:
        s.wait()
    ends = []
    total = 0
    for d in range(ndoc):
        total = total + doc_ref[d]
        ends.append(total)

    def doc_of(s):
        doc = jnp.int32(0)
        for e in ends:
            doc = doc + jnp.where(s >= e, 1, 0).astype(jnp.int32)
        return doc

    s0 = ord_ref[me]
    d0 = doc_of(s0)

    def earlier(k):
        want = s0 - k
        if nc <= 8:
            at = me
            for b in range(nc):
                at = jnp.where(ord_ref[b] == want, b, at)
        else:
            at = lax.fori_loop(
                0, nc, lambda b, at: jnp.where(ord_ref[b] == want, b, at), me)
        kept = (want >= 0) & (doc_of(want) == d0) & (k > 0)
        return at, jnp.where(kept, 0.0, MASKED).astype(jnp.float32)

    scale = HEAD_SIZE ** -0.5 * LOG2E
    tile = 2 * BLOCK_TOKENS
    col = lax.broadcasted_iota(jnp.int32, (tile, BLOCK_TOKENS), 1)
    row = lax.broadcasted_iota(jnp.int32, (tile, BLOCK_TOKENS), 0)
    inside = row - jnp.where(row >= BLOCK_TOKENS, BLOCK_TOKENS, 0)
    causal = jnp.where(col <= inside, 0.0, MASKED).astype(jnp.float32)
    ones = jnp.ones((GROUP_BLOCKS * BLOCK_TOKENS, D), jnp.bfloat16)

    def attend(h, places, first, last):
        k4 = jnp.concatenate([buf(h, 0)[b] for b, _ in places], axis=0)
        v4 = jnp.concatenate([buf(h, 1)[b] for b, _ in places], axis=0)
        v4 = jnp.concatenate([v4, ones[:v4.shape[0]]], axis=1)
        for t in range(group // 2):
            hq = h * group + 2 * t
            q2 = jnp.concatenate(
                [q_v[:, hq * D:(hq + 1) * D], q_v[:, (hq + 1) * D:(hq + 2) * D]], axis=0)
            s = lax.dot_general(
                q2, k4, (((1,), (1,)), ((), ())), preferred_element_type=jnp.float32)
            parts = [s[:, i * BLOCK_TOKENS:(i + 1) * BLOCK_TOKENS] * scale + bias
                     for i, (_, bias) in enumerate(places)]
            top = parts[0]
            for part in parts[1:]:
                top = jnp.maximum(top, part)
            top = jnp.max(top, axis=1, keepdims=True)
            rows = pl.ds(hq * BLOCK_TOKENS, tile)
            if not first:
                old = m_s[rows, 0:1]
                top = jnp.maximum(old, top)
            p = jnp.concatenate(
                [jnp.exp2(part - top).astype(jnp.bfloat16) for part in parts], axis=1)
            pv = jnp.dot(p, v4, preferred_element_type=jnp.float32)
            if not first:
                pv = acc[rows, :] * jnp.exp2(old - top) + pv
            if last:
                out = (pv[:, :D] / pv[:, D:]).astype(jnp.bfloat16)
                att[:, hq * D:(hq + 1) * D] = out[:BLOCK_TOKENS]
                att[:, (hq + 1) * D:(hq + 2) * D] = out[BLOCK_TOKENS:]
            else:
                acc[rows, :] = pv
                m_s[rows, :] = jnp.broadcast_to(top, (tile, D))

    def final_waits(h):
        def level(zb):
            b = zb * 2 + (1 - x)
            over_x(b, h, 1).wait_recv()
            if isinstance(zb, int):
                if 0 < zb < cz - 1:
                    over_x(b, h, 0).wait_recv()
            else:
                pl.when(jnp.logical_not(is_end(zb)))(lambda: over_x(b, h, 0).wait_recv())
        each(0, cz, level)
        for side in (1, -1):
            cross(cz - 1, h, side, start, True)

    near = min(GROUP_BLOCKS, span)
    spots = [(me, causal)] + [earlier(k) for k in range(1, near)]
    q_copy.wait()
    for h in range(heads_kv):
        final_waits(h)
        attend(h, spots, True, span <= near)
        if span > near:
            assert span % near == 0

            @pl.loop(1, span // near - 1)
            def _(g):
                attend(h, [earlier(g * near + k) for k in range(near)], False, False)

            attend(h, [earlier(span - near + k) for k in range(near)], False, True)

    strip = BLOCK_TOKENS // 4

    def c_copy(c):
        return pltpu.make_async_remote_copy(
            src_ref=p_v.at[c, 1 - core], dst_ref=r1.at[c],
            send_sem=c_send.at[c], recv_sem=c_recv.at[c],
            device_id={"tp": sib}, device_id_type=MESH)

    def y_copy(c):
        return pltpu.make_async_remote_copy(
            src_ref=s2.at[c], dst_ref=r2.at[c],
            send_sem=y_send.at[c], recv_sem=y_recv.at[c],
            device_id={"tp": ypeer}, device_id_type=MESH)

    def stage1(c):
        w_copy(c).wait()
        part = jnp.dot(att[...], w_v[c], preferred_element_type=jnp.float32)
        part = part.astype(jnp.bfloat16)
        for t in range(4):
            p_v[c, t % 2, t // 2] = part[t * strip:(t + 1) * strip]
        c_copy(c).start()

    def stage2(c):
        c_copy(c).wait_recv()
        s2[c] = (p_v[c, core, 1 - yy].astype(jnp.float32)
                 + r1[c, 1 - yy].astype(jnp.float32)).astype(jnp.bfloat16)
        y_copy(c).start()

    def stage3(c):
        y_copy(c).wait_recv()
        o_ref[:, c * width:(c + 1) * width] = (
            p_v[c, core, yy].astype(jnp.float32) + r1[c, yy].astype(jnp.float32)
            + r2[c].astype(jnp.float32)).astype(jnp.bfloat16)

    def drain():
        for h, c in pieces:
            pl.when(has_up)(lambda: sent(along(me, h, c, -1)))
            pl.when(has_dn)(lambda: sent(along(me, h, c, 1)))
            sent(over_x(me, h, c))
        each(1, cz, lambda d: relay(d, sent, sent, False))

    lag2, lag3 = 2, 6
    for i in range(chunks + lag3):
        if i < chunks:
            stage1(i)
        if 0 <= i - lag2 < chunks:
            stage2(i - lag2)
        if i == chunks + lag2:
            drain()
        if 0 <= i - lag3 < chunks:
            stage3(i - lag3)

    for c in range(chunks):
        c_copy(c).wait_send()
        y_copy(c).wait_send()


def local_fn(nc, queries, keys, values, doc_blocks, block_order, out_weight):
    rows, qcols = queries.shape
    depth, cols = out_weight.shape
    heads_kv = keys.shape[1] // HEAD_SIZE
    chunks = 8
    width = cols // chunks
    strip = rows // 4
    bf, f32 = jnp.bfloat16, jnp.float32
    dma = pltpu.SemaphoreType.DMA
    hbm = pl.BlockSpec(memory_space=pltpu.HBM)
    long = nc // 2 > GROUP_BLOCKS
    operands = [pltpu.with_memory_space_constraint(a, pltpu.HBM) for a in (
        queries, keys, values, doc_blocks, block_order, out_weight)]
    return pl.pallas_call(
        functools.partial(kernel, nc, doc_blocks.shape[0], chunks, heads_kv),
        out_shape=jax.ShapeDtypeStruct((strip, cols), bf),
        in_specs=[hbm] * 6,
        out_specs=pl.BlockSpec(memory_space=pltpu.VMEM),
        scratch_shapes=[
            pltpu.SMEM(doc_blocks.shape, jnp.int32),
            pltpu.SMEM(block_order.shape, jnp.int32),
            pltpu.VMEM((chunks, depth, width), bf),
            pltpu.VMEM((rows, qcols), bf),
            pltpu.VMEM((rows, qcols), bf),
            pltpu.VMEM((chunks, 2, 2, strip, width), bf),
            pltpu.VMEM((chunks, 2, strip, width), bf),
            pltpu.VMEM((chunks, strip, width), bf),
            pltpu.VMEM((chunks, strip, width), bf),
            pltpu.VMEM((qcols if long else 8, HEAD_SIZE), f32),
            pltpu.VMEM((qcols if long else 8, 2 * HEAD_SIZE), f32),
            dma((2,)), dma((heads_kv, 2)), dma, dma((chunks,)),
            dma((nc, heads_kv, 2)), dma((nc, heads_kv, 2)), dma((nc, heads_kv, 2)),
            dma((nc, heads_kv, 2)),
            dma((chunks,)), dma((chunks,)), dma((chunks,)), dma((chunks,)),
        ] + [pltpu.VMEM((nc, BLOCK_TOKENS, HEAD_SIZE), bf)] * (2 * heads_kv),
        compiler_params=pltpu.CompilerParams(
            collective_id=0, has_side_effects=True, vmem_limit_bytes=48 * 2**20),
    )(*operands)


def solution(mesh):
    placed = (P("cp", "tp"), P("cp", "tp"), P("cp", "tp"), P(), P(), P("tp", None))
    assert mesh.shape["tp"] == 4
    return jax.shard_map(
        functools.partial(local_fn, mesh.shape["cp"]),
        mesh=mesh, in_specs=placed, out_specs=P(("cp", "tp"), None), check_vma=False,
    )
```

time: 39.8 us -> 31.3 us (0.79)
  Pallas kernels: 37.9 us -> 30.4 us
  local copies, waits for them, and re-layouts: 1.67 us -> 0.71 us
    pallas_call x1, Pallas kernels: 37.9 us -> 30.4 us  [local_fn(): pl.pallas_call(functools.partial(kernel, nc, doc_blocks.shape[0], chunks,...]
    unnamed x1, local copies, waits for them, and re-layouts: 1.67 us -> 0.71 us
where the time goes in v2:
time: 31.3 us; the launch traced here: 31.1 us
  Pallas kernels  30.4 us (97%)
  local copies, waits for them, and re-layouts  0.71 us (2%)
    pallas_call x1, Pallas kernels, local_fn(): pl.pallas_call(functools.partial(kernel, nc, doc_blocks.shape[0], chunks,...  30.4 us
    unnamed x1, local copies, waits for them, and re-layouts  0.71 us

profile of v2, /device:TPU:0, one launch (start us, length us, event | category | flops | bytes accessed | tf_op | source)
XLA Modules:
  0.0 31.1 jit_solution(14093618105387045498)
XLA Ops:
  0.0 30.4 %shard_map.64 = bf16[32,4096]{1,0:T(8,128)(2,1)S(1)} custom-call(bf16[128,2048]{1,0:T(8,128)(2,1)} %q_hbm.1, bf16[128,256]{1,0:T(8,128)(2,1)} %k_hbm.1, bf16[128,256]{1,0:T(8,128)(2,1)} %v_hbm.1, s32[4]{0:T(128)} %doc_hbm.1, s32[8]{0:T(128)} %ord_hbm.1, bf16[2048,4096]{1,0:T(8,128)(2,1)} %w_hbm.1), custom_call_target="tpu_custom_call" | custom-call | tf_op jit(solution)/shard_map/pallas_call | solution.py:319
  30.4 0.7 %copy.8 = bf16[32,4096]{1,0:T(8,128)(2,1)} copy(bf16[32,4096]{1,0:T(8,128)(2,1)S(1)} %shard_map.64) | data formatting | bytes 524288
